TPU v7x, 32 devices: a whole 2x2x4 slice. The times are simulated.
32 devices in a mesh: mp: 8 (over z, y), dp: 4 (over x, core).
Axes of the slice: x: 2, y: 2, z: 4, core: 2. Of those that a mesh axis runs over, the one named last changes fastest.
Arguments:
- features: bfloat16 [32, 4, 4, 512], P(('dp', 'mp')), may hold values from 0 to 2
- labels: int32 [32], P('dp'), may hold values from 0 to 9
- subset_ids: int32 [8], P('mp'), may hold values from 0 to 255
- conv1_weight: bfloat16 [8, 9, 512, 512], P('mp'), may hold values from -0.09375 to 0.09375
- conv2_weight: bfloat16 [8, 9, 512, 512], P('mp'), may hold values from -0.09375 to 0.09375
- head_weight: float32 [8, 512, 10], P('mp'), may hold values from -0.25 to 0.25
Outputs:
- datamodel: float32 [32, 256], P(('dp', 'mp'))
- margin_mean: float32 [32], P(('dp', 'mp'))
- margin_norm: float32 [32], P(('dp', 'mp'))
All inputs are finite; a program needn't handle non-finite values.
Results may differ from a plain program's by a relative error of at most 0.00077.
Values may be sent and summed in bfloat16 or wider, within the bound.
A program may use at most 128 MiB of HBM per device.

v0:
```python
import jax
import jax.numpy as jnp
from jax import lax
from jax.sharding import PartitionSpec as P

SUBSETS = 256


def convolve(grid, kernel):
    batch = grid.shape[0]
    width = grid.shape[1]
    chans = grid.shape[3]
    padded = jnp.pad(grid, ((0, 0), (1, 1), (1, 1), (0, 0)))
    result = jnp.zeros((batch * width * width, kernel.shape[2]), jnp.float32)
    for offset in range(9):
        row_off, col_off = divmod(offset, 3)
        shifted = padded[:, row_off : row_off + width, col_off : col_off + width, :].reshape(
            batch * width * width, chans
        )
        result = result + jnp.dot(shifted, kernel[offset], preferred_element_type=jnp.float32)
    return result


def margins_of(grid, first_kernel, second_kernel, head, target_labels):
    batch = grid.shape[0]
    width = grid.shape[1]
    chans = grid.shape[3]
    hidden = (
        jax.nn.relu(convolve(grid, first_kernel))
        .astype(jnp.bfloat16)
        .reshape(batch, width, width, chans)
    )
    branch = jax.nn.relu(convolve(hidden, second_kernel))
    blocked = grid.astype(jnp.float32).reshape(batch * width * width, chans) + branch
    pooled = jnp.max(blocked.reshape(batch, width * width, chans), axis=1)
    logits = jnp.dot(
        pooled, head, precision=lax.Precision.HIGHEST, preferred_element_type=jnp.float32
    )
    classes = jnp.arange(head.shape[1], dtype=jnp.int32)[None, :]
    chosen = classes == target_labels[:, None]
    correct = jnp.sum(jnp.where(chosen, logits, 0.0), axis=1)
    rival = jnp.max(jnp.where(chosen, -1e30, logits), axis=1)
    return correct - rival


def subset_table(identity):
    return (identity[:, None] == jnp.arange(SUBSETS, dtype=jnp.int32)[None, :]).astype(jnp.float32)


def shards(features, labels, subset_ids, conv1_weight, conv2_weight, head_weight):
    models_dev = conv1_weight.shape[0]
    model_count = models_dev * lax.axis_size("mp")
    rows_out = [
        margins_of(
            lax.all_gather(features, "mp", axis=0, tiled=True),
            conv1_weight[0],
            conv2_weight[0],
            head_weight[0],
            labels,
        )
    ]
    margin = jnp.stack(rows_out, 0)
    columns = lax.all_to_all(margin, "mp", split_axis=1, concat_axis=0, tiled=True)
    every_id = lax.all_gather(subset_ids, "mp", axis=0, tiled=True)
    margin_mean = jnp.sum(columns, axis=0) / model_count
    centred = columns - margin_mean[None, :]
    margin_norm = jnp.sqrt(1.0 + jnp.sum(centred * centred, axis=0) / model_count)
    scaled = centred / margin_norm[None, :]
    datamodel = jnp.dot(
        scaled.T,
        subset_table(every_id),
        precision=lax.Precision.HIGHEST,
        preferred_element_type=jnp.float32,
    )
    return (datamodel, margin_mean, margin_norm)


def solution(mesh):
    in_specs = (
        P(("dp", "mp"), None, None, None),
        P("dp"),
        P("mp"),
        P("mp", None, None, None),
        P("mp", None, None, None),
        P("mp", None, None),
    )
    out_specs = (P(("dp", "mp"), None), P(("dp", "mp")), P(("dp", "mp")))
    return jax.shard_map(shards, mesh=mesh, in_specs=in_specs, out_specs=out_specs, check_vma=False)
```

profile of v0, /device:TPU:0, one launch (start us, length us, event | category | flops | bytes accessed | tf_op | source)
XLA Modules:
  0.0 84.1 jit_solution(346595920201907699)
XLA Ops:
  0.6 32.5 %all_gather.6 = bf16[8,4,4,512]{3,2,1,0:T(4,128)(2,1)S(1)} all-gather(bf16[1,4,4,512]{3,2,1,0:T(4,128)(2,1)} %param.6), channel_id=1, replica_groups=mesh['mp'=8,'dp'=4] {'mp'}, dimensions={0}, use_global_device_ids=true | all-gather | bytes 147456 | tf_op jit(solution)/shard_map/all_gather | solution.py:55
  33.2 0.5 pad_slice_fusion.8
  34.0 1.3 %fusion.22 = f32[128,512]{1,0:T(8,128)S(1)} fusion(bf16[128,512]{1,0:T(8,128)(2,1)S(1)} %reshape.174, bf16[1,9,512,512]{3,2,1,0:T(8,128)(2,1)} %param.9), kind=kOutput, calls=%fused_computation.54 | convolution fusion | flops 67108864 | bytes 917504 | tf_op jit(solution)/shard_map/dot_general | solution.py:20
  35.3 1.3 %convolution_add_fusion.15 = f32[128,512]{1,0:T(8,128)S(1)} fusion(f32[128,512]{1,0:T(8,128)S(1)} %fusion.22, bf16[128,512]{1,0:T(8,128)(2,1)S(1)} %reshape.175, bf16[1,9,512,512]{3,2,1,0:T(8,128)(2,1)} %param.9), kind=kOutput, calls=%fused_computation.15 | convolution fusion | flops 67174400 | bytes 1179648 | tf_op jit(solution)/shard_map/dot_general | solution.py:20
  36.6 1.3 %convolution_add_fusion.14 = f32[128,512]{1,0:T(8,128)S(1)} fusion(f32[128,512]{1,0:T(8,128)S(1)} %convolution_add_fusion.15, bf16[128,512]{1,0:T(8,128)(2,1)S(1)} %reshape.176, bf16[1,9,512,512]{3,2,1,0:T(8,128)(2,1)} %param.9), kind=kOutput, calls=%fused_computation.14 | convolution fusion | flops 67174400 | bytes 1179648 | tf_op jit(solution)/shard_map/dot_general | solution.py:20
  37.9 1.3 %convolution_add_fusion.13 = f32[128,512]{1,0:T(8,128)S(1)} fusion(f32[128,512]{1,0:T(8,128)S(1)} %convolution_add_fusion.14, bf16[128,512]{1,0:T(8,128)(2,1)S(1)} %reshape.177, bf16[1,9,512,512]{3,2,1,0:T(8,128)(2,1)} %param.9), kind=kOutput, calls=%fused_computation.13 | convolution fusion | flops 67174400 | bytes 1179648 | tf_op jit(solution)/shard_map/dot_general | solution.py:20
  39.1 1.3 %convolution_add_fusion.12 = f32[128,512]{1,0:T(8,128)S(1)} fusion(f32[128,512]{1,0:T(8,128)S(1)} %convolution_add_fusion.13, bf16[128,512]{1,0:T(8,128)(2,1)S(1)} %reshape.172, bf16[1,9,512,512]{3,2,1,0:T(8,128)(2,1)} %param.9), kind=kOutput, calls=%fused_computation.12 | convolution fusion | flops 67174400 | bytes 1179648 | tf_op jit(solution)/shard_map/dot_general | solution.py:20
  40.4 1.3 %convolution_add_fusion.11 = f32[128,512]{1,0:T(8,128)S(1)} fusion(f32[128,512]{1,0:T(8,128)S(1)} %convolution_add_fusion.12, bf16[128,512]{1,0:T(8,128)(2,1)S(1)} %reshape.178, bf16[1,9,512,512]{3,2,1,0:T(8,128)(2,1)} %param.9), kind=kOutput, calls=%fused_computation.11 | convolution fusion | flops 67174400 | bytes 1179648 | tf_op jit(solution)/shard_map/dot_general | solution.py:20
  41.7 1.3 %convolution_add_fusion.10 = f32[128,512]{1,0:T(8,128)S(1)} fusion(f32[128,512]{1,0:T(8,128)S(1)} %convolution_add_fusion.11, bf16[128,512]{1,0:T(8,128)(2,1)S(1)} %reshape.179, bf16[1,9,512,512]{3,2,1,0:T(8,128)(2,1)} %param.9), kind=kOutput, calls=%fused_computation.10 | convolution fusion | flops 67174400 | bytes 1179648 | tf_op jit(solution)/shard_map/dot_general | solution.py:20
  43.0 1.3 %convolution_add_fusion.9 = f32[128,512]{1,0:T(8,128)S(1)} fusion(f32[128,512]{1,0:T(8,128)S(1)} %convolution_add_fusion.10, bf16[128,512]{1,0:T(8,128)(2,1)S(1)} %reshape.180, bf16[1,9,512,512]{3,2,1,0:T(8,128)(2,1)} %param.9), kind=kOutput, calls=%fused_computation.9 | convolution fusion | flops 67174400 | bytes 1179648 | tf_op jit(solution)/shard_map/dot_general | solution.py:20
  44.3 1.3 %fusion.3 = bf16[128,512]{1,0:T(8,128)(2,1)S(1)} fusion(f32[128,512]{1,0:T(8,128)S(1)} %convolution_add_fusion.9, bf16[128,512]{1,0:T(8,128)(2,1)S(1)} %reshape.181, bf16[1,9,512,512]{3,2,1,0:T(8,128)(2,1)} %param.9), kind=kOutput, calls=%fused_computation.19 | convolution fusion | flops 67305472 | bytes 1048576 | tf_op jit(solution)/shard_map/dot_general | solution.py:20
  45.6 0.5 pad_slice_fusion
  46.2 1.3 %fusion.12 = f32[128,512]{1,0:T(8,128)S(1)} fusion(bf16[128,512]{1,0:T(8,128)(2,1)S(1)} %reshape.183, bf16[1,9,512,512]{3,2,1,0:T(8,128)(2,1)} %param.10), kind=kOutput, calls=%fused_computation.44 | convolution fusion | flops 67108864 | bytes 917504 | tf_op jit(solution)/shard_map/dot_general | solution.py:20
  47.5 1.3 %convolution_add_fusion.7 = f32[128,512]{1,0:T(8,128)S(1)} fusion(f32[128,512]{1,0:T(8,128)S(1)} %fusion.12, bf16[128,512]{1,0:T(8,128)(2,1)S(1)} %reshape.184, bf16[1,9,512,512]{3,2,1,0:T(8,128)(2,1)} %param.10), kind=kOutput, calls=%fused_computation.7 | convolution fusion | flops 67174400 | bytes 1179648 | tf_op jit(solution)/shard_map/dot_general | solution.py:20
  48.8 0.0 copy-start
  48.8 0.0 copy-start.1
  48.8 0.0 copy-start.2
  48.8 1.3 %convolution_add_fusion.6 = f32[128,512]{1,0:T(8,128)S(1)} fusion(f32[128,512]{1,0:T(8,128)S(1)} %convolution_add_fusion.7, bf16[128,512]{1,0:T(8,128)(2,1)S(1)} %reshape.185, bf16[1,9,512,512]{3,2,1,0:T(8,128)(2,1)} %param.10), kind=kOutput, calls=%fused_computation.6 | convolution fusion | flops 67174400 | bytes 1179648 | tf_op jit(solution)/shard_map/dot_general | solution.py:20
  50.1 1.3 %convolution_add_fusion.5 = f32[128,512]{1,0:T(8,128)S(1)} fusion(f32[128,512]{1,0:T(8,128)S(1)} %convolution_add_fusion.6, bf16[128,512]{1,0:T(8,128)(2,1)S(1)} %reshape.186, bf16[1,9,512,512]{3,2,1,0:T(8,128)(2,1)} %param.10), kind=kOutput, calls=%fused_computation.5 | convolution fusion | flops 67174400 | bytes 1179648 | tf_op jit(solution)/shard_map/dot_general | solution.py:20
  51.4 1.3 %convolution_add_fusion.4 = f32[128,512]{1,0:T(8,128)S(1)} fusion(f32[128,512]{1,0:T(8,128)S(1)} %convolution_add_fusion.5, bf16[128,512]{1,0:T(8,128)(2,1)S(1)} %fusion.3, bf16[1,9,512,512]{3,2,1,0:T(8,128)(2,1)} %param.10), kind=kOutput, calls=%fused_computation.4 | convolution fusion | flops 67174400 | bytes 1179648 | tf_op jit(solution)/shard_map/dot_general | solution.py:20
  52.8 1.3 %convolution_add_fusion.3 = f32[128,512]{1,0:T(8,128)S(1)} fusion(f32[128,512]{1,0:T(8,128)S(1)} %convolution_add_fusion.4, bf16[128,512]{1,0:T(8,128)(2,1)S(1)} %reshape.187, bf16[1,9,512,512]{3,2,1,0:T(8,128)(2,1)} %param.10), kind=kOutput, calls=%fused_computation.3 | convolution fusion | flops 67174400 | bytes 1179648 | tf_op jit(solution)/shard_map/dot_general | solution.py:20
  54.1 1.3 %convolution_add_fusion.2 = f32[128,512]{1,0:T(8,128)S(1)} fusion(f32[128,512]{1,0:T(8,128)S(1)} %convolution_add_fusion.3, bf16[128,512]{1,0:T(8,128)(2,1)S(1)} %reshape.188, bf16[1,9,512,512]{3,2,1,0:T(8,128)(2,1)} %param.10), kind=kOutput, calls=%fused_computation.2 | convolution fusion | flops 67174400 | bytes 1179648 | tf_op jit(solution)/shard_map/dot_general | solution.py:20
  55.4 1.3 %convolution_add_fusion.1 = f32[128,512]{1,0:T(8,128)S(1)} fusion(f32[128,512]{1,0:T(8,128)S(1)} %convolution_add_fusion.2, bf16[128,512]{1,0:T(8,128)(2,1)S(1)} %reshape.189, bf16[1,9,512,512]{3,2,1,0:T(8,128)(2,1)} %param.10), kind=kOutput, calls=%fused_computation.1 | convolution fusion | flops 67174400 | bytes 1179648 | tf_op jit(solution)/shard_map/dot_general | solution.py:20
  56.7 1.3 %bitcast_reduce_fusion = f32[8,512]{1,0:T(8,128)S(1)} fusion(f32[128,512]{1,0:T(8,128)S(1)} %convolution_add_fusion.1, bf16[128,512]{1,0:T(8,128)(2,1)S(1)} %reshape.190, bf16[1,9,512,512]{3,2,1,0:T(8,128)(2,1)} %param.10, bf16[128,512]{1,0:T(8,128)(2,1)S(1)} %reshape.172), kind=kOutput, calls=%fused_computation.74 | convolution fusion | flops 67432448 | bytes 1064960 | tf_op jit(solution)/shard_map/dot_general | solution.py:20
  58.0 0.0 copy-done
  58.0 0.0 copy-done.1
  58.0 0.3 select_reduce_fusion
  58.3 0.7 copy.10
  59.6 0.0 copy-done.2
  59.6 0.6 dynamic-slice
  60.2 0.8 dynamic-update-slice
  61.0 5.5 %all-to-all-start = ((f32[1,8,1]{2,0,1:T(1,128)}), f32[1,8,1]{2,0,1:T(1,128)S(1)}, u32[]{:S(2)}, u32[]{:S(2)}) async-start(f32[1,8,1]{2,0,1:T(1,128)} %copy.10), calls=%async_computation | async-start | bytes 8192 | tf_op jit(solution)/shard_map/all_to_all | solution.py:63
  66.5 11.9 %all-reduce.2 = s32[8]{0:T(128)S(1)} all-reduce(s32[8]{0:T(128)S(1)} %dynamic-update-slice), channel_id=1, replica_groups=mesh['mp'=8,'dp'=4] {'mp'}, use_global_device_ids=true, to_apply=%add.2 | all-reduce | flops 8 | bytes 64
  78.4 0.0 all-to-all-done
  78.4 0.6 reduce_sum.28
  79.6 0.6 multiply_reduce_fusion
  80.9 0.1 divide_reduce_fusion
  81.1 0.8 fusion.47
  (20 shorter events, 0.7 us)
Async XLA Ops:
  48.8 9.2 %copy-start = (f32[1,512,10]{1,0,2:T(1,128)S(1)}, f32[1,512,10]{1,0,2:T(1,128)}, u32[]{:S(2)}) copy-start(f32[1,512,10]{1,0,2:T(1,128)} %param.11) | copy-start | bytes 61444
  48.8 9.2 %copy-start.1 = (s32[8]{0:T(128)S(1)}, s32[8]{0:T(128)}, u32[]{:S(2)}) copy-start(s32[8]{0:T(128)} %param.7) | copy-start | bytes 100
  48.8 10.8 %copy-start.2 = (u32[32]{0:T(128)S(1)}, u32[32]{0:T(128)}, u32[]{:S(2)}) copy-start(u32[32]{0:T(128)} %constant.32) | copy-start | bytes 388
  61.0 17.4 %all-to-all-start = ((f32[1,8,1]{2,0,1:T(1,128)}), f32[1,8,1]{2,0,1:T(1,128)S(1)}, u32[]{:S(2)}, u32[]{:S(2)}) async-start(f32[1,8,1]{2,0,1:T(1,128)} %copy.10), calls=%async_computation | async-start | bytes 8192 | tf_op jit(solution)/shard_map/all_to_all | solution.py:63
where the time goes:
time: 85.2 us; the launch traced here: 84.1 us
  blocking collectives  44.4 us (52%)
  matrix products  24 us (28%)
  starting transfers between devices  5.52 us (6%)
  between operations  5.14 us (6%)
  local copies, waits for them, and re-layouts  3.67 us (4%)
  other arithmetic  1.37 us (2%)
    all_gather x1, blocking collectives, shards(): lax.all_gather(features, 'mp', axis=0, tiled=True)  32.5 us
    dot_general x18, matrix products, convolve(): jnp.dot(shifted, kernel[offset], preferred_element_type=jnp.float32)  23 us
    unnamed x1, blocking collectives  11.9 us
    all_to_all x1, starting transfers between devices, shards(): lax.all_to_all(margin, 'mp', split_axis=1, concat_axis=0, tiled=True)  5.52 us
  transfers between devices with their start and end apart: 1, of which 0 were waited for; matrix products, arithmetic and copies ran while one was open for 0% of the time, Pallas kernels for 0%

commit v1 on v0

v1 whole, which is shorter than its diff:
```python
import functools

import jax
import jax.numpy as jnp
from jax import lax
from jax.experimental import pallas as pl
from jax.experimental.pallas import tpu as pltpu
from jax.sharding import PartitionSpec as P

SUBSETS = 256
GROUP = 8
LANES = 128
MESH = pl.DeviceIdType.MESH


def kernel(
    n, feat_ref, labels_ref, ids_ref, w1_ref, w2_ref, head_ref,
    data_ref, mean_ref, norm_ref,
    gathered, w1, w2, head, lhs, msg, got,
    own_sem, w1_sem, w2_sem, head_sem, fsend, frecv, msend, mrecv,
):
    me = lax.axis_index("mp")
    width = feat_ref.shape[1]
    chans = feat_ref.shape[3]
    spots = width * width
    rows = GROUP * spots
    offsets = w1_ref.shape[1]
    classes = head_ref.shape[0]

    own = pltpu.make_async_copy(feat_ref.at[0], gathered.at[me], own_sem)
    own.start()
    w1_copies = [
        pltpu.make_async_copy(w1_ref.at[0, o], w1.at[o], w1_sem.at[o]) for o in range(offsets)
    ]
    w2_copies = [
        pltpu.make_async_copy(w2_ref.at[0, o], w2.at[o], w2_sem.at[o]) for o in range(offsets)
    ]
    head_copy = pltpu.make_async_copy(head_ref, head, head_sem)

    peers = [lax.rem(me + j, n) for j in range(1, n)]
    barrier = pltpu.get_barrier_semaphore()
    for peer in peers:
        pl.semaphore_signal(barrier, inc=1, device_id={"mp": peer}, device_id_type=MESH)
    for copy in w1_copies:
        copy.start()
    for copy in w2_copies:
        copy.start()
    head_copy.start()

    r = lax.broadcasted_iota(jnp.int32, (rows, rows), 0)
    c = lax.broadcasted_iota(jnp.int32, (rows, rows), 1)
    source = lax.rem(r, GROUP) * spots + lax.div(r, GROUP)
    reorder = jnp.where(c == source, 1.0, 0.0).astype(jnp.bfloat16)
    sub = lax.broadcasted_iota(jnp.int32, (GROUP, 1), 0)
    identity = ids_ref[0].astype(jnp.float32)
    for t in range(n):
        msg[t, 1:2, :] = jnp.full((1, LANES), identity, jnp.float32)

    own.wait()
    pl.semaphore_wait(barrier, n - 1)
    feature_sends = []
    for j, peer in enumerate(peers):
        copy = pltpu.make_async_remote_copy(
            src_ref=gathered.at[me], dst_ref=gathered.at[me],
            send_sem=fsend.at[j], recv_sem=frecv.at[me],
            device_id={"mp": peer}, device_id_type=MESH,
        )
        copy.start()
        feature_sends.append(copy)

    for copy in w1_copies:
        copy.wait()
    for copy in w2_copies:
        copy.wait()
    head_copy.wait()
    for peer in peers:
        pltpu.make_async_remote_copy(
            src_ref=gathered.at[peer], dst_ref=gathered.at[peer],
            send_sem=fsend.at[0], recv_sem=frecv.at[peer],
            device_id={"mp": peer}, device_id_type=MESH,
        ).wait_recv()

    def convolve(grid, kernel_ref):
        blank = jnp.zeros((GROUP, chans), jnp.float32)
        for o in range(offsets):
            dy, dx = o // 3 - 1, o % 3 - 1
            blocks = []
            for y in range(width):
                for x in range(width):
                    inside = 0 <= y + dy < width and 0 <= x + dx < width
                    q = ((y + dy) * width + x + dx) * GROUP
                    blocks.append(grid[q : q + GROUP] if inside else blank)
            lhs[:, o * chans : (o + 1) * chans] = jnp.concatenate(blocks, 0).astype(jnp.bfloat16)
        return jnp.dot(
            lhs[...],
            kernel_ref[...].reshape(offsets * chans, chans),
            preferred_element_type=jnp.float32,
        )

    def group(first):
        raw = gathered[pl.ds(first, GROUP)].astype(jnp.float32).reshape(rows, chans)
        grid = jnp.dot(reorder, raw.astype(jnp.bfloat16), preferred_element_type=jnp.float32)
        hidden = jnp.maximum(convolve(grid, w1), 0.0)
        block = grid + jnp.maximum(convolve(hidden, w2), 0.0)
        pooled = block[:GROUP]
        for p in range(1, spots):
            pooled = jnp.maximum(pooled, block[p * GROUP : (p + 1) * GROUP])
        label = jnp.zeros((GROUP, 1), jnp.int32)
        for t in range(GROUP):
            label = jnp.where(sub == t, labels_ref[first + t], label)
        correct = jnp.zeros((GROUP, 1), jnp.float32)
        rival = jnp.full((GROUP, 1), -1e30, jnp.float32)
        for k in range(classes):
            logit = jnp.sum(pooled * head[k], axis=1, keepdims=True)
            correct = jnp.where(label == k, logit, correct)
            rival = jnp.where(label == k, rival, jnp.maximum(rival, logit))
        margin = jnp.broadcast_to(correct - rival, (GROUP, LANES))
        for t in range(GROUP):
            msg[first + t, 0:1, :] = margin[t : t + 1]

    if n == GROUP:
        group(0)
    else:
        pl.loop(0, n // GROUP)(lambda g: group(g * GROUP))

    margin_sends = []
    for j, peer in enumerate(peers):
        copy = pltpu.make_async_remote_copy(
            src_ref=msg.at[peer], dst_ref=got.at[me],
            send_sem=msend.at[j], recv_sem=mrecv.at[me],
            device_id={"mp": peer}, device_id_type=MESH,
        )
        copy.start()
        margin_sends.append(copy)
    got[me] = msg[me]
    for copy in feature_sends:
        copy.wait_send()
    for copy in margin_sends:
        copy.wait_send()
    for peer in peers:
        pltpu.make_async_remote_copy(
            src_ref=msg.at[peer], dst_ref=got.at[peer],
            send_sem=msend.at[0], recv_sem=mrecv.at[peer],
            device_id={"mp": peer}, device_id_type=MESH,
        ).wait_recv()

    total = got[0, 0:1, :]
    for m in range(1, n):
        total = total + got[m, 0:1, :]
    mean = total / n
    spread = jnp.zeros_like(mean)
    for m in range(n):
        centred = got[m, 0:1, :] - mean
        spread = spread + centred * centred
    norm = jnp.sqrt(1.0 + spread / n)
    lane = lax.broadcasted_iota(jnp.int32, (1, LANES), 1).astype(jnp.float32)
    for start in range(0, SUBSETS, LANES):
        acc = jnp.zeros((1, LANES), jnp.float32)
        for m in range(n):
            scaled = (got[m, 0:1, :] - mean) / norm
            acc = acc + jnp.where(got[m, 1:2, :] == lane + start, scaled, 0.0)
        data_ref[:, start : start + LANES] = acc
    mean_ref[...] = mean[0, :1]
    norm_ref[...] = norm[0, :1]


def shards(n, features, labels, subset_ids, conv1_weight, conv2_weight, head_weight):
    width, chans = features.shape[1], features.shape[3]
    offsets = conv1_weight.shape[1]
    assert features.shape[0] == 1 and conv1_weight.shape[0] == 1 and n % GROUP == 0
    head = jnp.transpose(head_weight, (2, 0, 1))
    anywhere = pl.BlockSpec(memory_space=pl.ANY)
    smem = pl.BlockSpec(memory_space=pltpu.SMEM)
    vmem = pl.BlockSpec(memory_space=pltpu.VMEM)
    return pl.pallas_call(
        functools.partial(kernel, n),
        out_shape=(
            jax.ShapeDtypeStruct((1, SUBSETS), jnp.float32),
            jax.ShapeDtypeStruct((1,), jnp.float32),
            jax.ShapeDtypeStruct((1,), jnp.float32),
        ),
        in_specs=[anywhere, smem, smem, anywhere, anywhere, anywhere],
        out_specs=(vmem, vmem, vmem),
        scratch_shapes=[
            pltpu.VMEM((n, width, width, chans), features.dtype),
            pltpu.VMEM(conv1_weight.shape[1:], conv1_weight.dtype),
            pltpu.VMEM(conv2_weight.shape[1:], conv2_weight.dtype),
            pltpu.VMEM(head.shape, head.dtype),
            pltpu.VMEM((GROUP * width * width, offsets * chans), features.dtype),
            pltpu.VMEM((n, 2, LANES), jnp.float32),
            pltpu.VMEM((n, 2, LANES), jnp.float32),
            pltpu.SemaphoreType.DMA,
            pltpu.SemaphoreType.DMA((offsets,)),
            pltpu.SemaphoreType.DMA((offsets,)),
            pltpu.SemaphoreType.DMA,
            pltpu.SemaphoreType.DMA((n,)),
            pltpu.SemaphoreType.DMA((n,)),
            pltpu.SemaphoreType.DMA((n,)),
            pltpu.SemaphoreType.DMA((n,)),
        ],
        compiler_params=pltpu.CompilerParams(
            collective_id=0, has_side_effects=True, vmem_limit_bytes=60 * 1024 * 1024
        ),
    )(features, labels, subset_ids, conv1_weight, conv2_weight, head)


def solution(mesh):
    in_specs = (
        P(("dp", "mp"), None, None, None),
        P("dp"),
        P("mp"),
        P("mp", None, None, None),
        P("mp", None, None, None),
        P("mp", None, None),
    )
    out_specs = (P(("dp", "mp"), None), P(("dp", "mp")), P(("dp", "mp")))
    return jax.shard_map(
        functools.partial(shards, mesh.shape["mp"]),
        mesh=mesh, in_specs=in_specs, out_specs=out_specs, check_vma=False,
    )
```

time: 85.2 us -> 24.9 us (0.29)
  blocking collectives: 44.4 us -> 0 us
  matrix products: 24 us -> 0 us
  Pallas kernels: 0 us -> 18.5 us
  starting transfers between devices: 5.52 us -> 0 us
  local copies, waits for them, and re-layouts: 3.67 us -> 1.22 us
  other arithmetic: 1.37 us -> 0 us
    all_gather x1 -> x0, blocking collectives: 32.5 us -> none  [shards(): lax.all_gather(features, 'mp', axis=0, tiled=True)]
    dot_general x20 -> x0, matrix products: 24 us -> none  [the longest x18 23 us: convolve(): jnp.dot(shifted, kernel[offset], preferred_element_type=jnp.float32)]
    pallas_call x0 -> x1, Pallas kernels: none -> 18.5 us  [shards(): pl.pallas_call(functools.partial(kernel, n), out_shape=(jax.ShapeDtypeStr...]
    unnamed x1 -> x0, blocking collectives: 11.9 us -> none
    all_to_all x1 -> x0, starting transfers between devices: 5.52 us -> none  [shards(): lax.all_to_all(margin, 'mp', split_axis=1, concat_axis=0, tiled=True)]
    reduce_sum x2 -> x0, other arithmetic: 1.22 us -> none  [the longest x1 0.61 us: shards(): margin_mean = jnp.sum(columns, axis=0) / model_count]
    slice x2 -> x0, local copies, waits for them, and re-layouts: 0.96 us -> none  [convolve(): padded[:, row_off:row_off + width, col_off:col_off + width, :]]
  transfers between devices with their start and end apart: 1 -> 0, of which waited for: 0 -> 0; matrix products, arithmetic and copies ran while one was open for 0% -> 0% of each run, Pallas kernels for 0% -> 0%
where the time goes in v1:
time: 24.9 us; the launch traced here: 24.6 us
  Pallas kernels  18.5 us (74%)
  between operations  4.81 us (19%)
  local copies, waits for them, and re-layouts  1.22 us (5%)
    pallas_call x1, Pallas kernels, shards(): pl.pallas_call(functools.partial(kernel, n), out_shape=(jax.ShapeDtypeStr...  18.5 us
    unnamed x1, local copies, waits for them, and re-layouts  1.22 us

profile of v1, /device:TPU:0, one launch (start us, length us, event | category | flops | bytes accessed | tf_op | source)
XLA Modules:
  0.0 24.6 jit_solution(7932983405276309857)
XLA Ops:
  1.3 18.5 %shard_map.85 = (f32[1,256]{1,0:T(1,128)}, f32[1]{0:T(128)}, f32[1]{0:T(128)}) custom-call(bf16[1,4,4,512]{3,2,1,0:T(4,128)(2,1)} %feat_ref.1, s32[8]{0:T(128)} %labels_ref.1, s32[1]{0:T(128)S(6)} %copy.12.ids_ref, bf16[1,9,512,512]{3,2,1,0:T(8,128)(2,1)} %w1_ref.1, bf16[1,9,512,512]{3,2,1,0:T(8,128)(2,1)} %w2_ref.1, f32[10,1,512]{2,1,0:T(1,128)} %bitcast.1), custom_call_target="tpu_custom_call" | custom-call | tf_op jit(solution)/shard_map/pallas_call | solution.py:175
  19.8 1.2 %copy.13 = f32[1,256]{1,0:T(1,128)} copy(f32[1,256]{1,0:T(1,128)} %get-tuple-element.6) | data formatting | bytes 2048

commit v2 on v1

--- a/solution.py
+++ b/solution.py
@@ -16,8 +16,8 @@
 def kernel(
     n, feat_ref, labels_ref, ids_ref, w1_ref, w2_ref, head_ref,
     data_ref, mean_ref, norm_ref,
-    gathered, w1, w2, head, lhs, msg, got,
-    own_sem, w1_sem, w2_sem, head_sem, fsend, frecv, msend, mrecv,
+    gathered, labels, ids, w1, w2, head, lhs, msg, got,
+    small_sem, own_sem, w1_sem, w2_sem, head_sem, fsend, frecv, msend, mrecv,
 ):
     me = lax.axis_index("mp")
     width = feat_ref.shape[1]
@@ -29,6 +29,12 @@
 
     own = pltpu.make_async_copy(feat_ref.at[0], gathered.at[me], own_sem)
     own.start()
+    small_copies = [
+        pltpu.make_async_copy(labels_ref, labels, small_sem.at[0]),
+        pltpu.make_async_copy(ids_ref, ids, small_sem.at[1]),
+    ]
+    for copy in small_copies:
+        copy.start()
     w1_copies = [
         pltpu.make_async_copy(w1_ref.at[0, o], w1.at[o], w1_sem.at[o]) for o in range(offsets)
     ]
@@ -52,7 +58,9 @@
     source = lax.rem(r, GROUP) * spots + lax.div(r, GROUP)
     reorder = jnp.where(c == source, 1.0, 0.0).astype(jnp.bfloat16)
     sub = lax.broadcasted_iota(jnp.int32, (GROUP, 1), 0)
-    identity = ids_ref[0].astype(jnp.float32)
+    for copy in small_copies:
+        copy.wait()
+    identity = ids[0].astype(jnp.float32)
     for t in range(n):
         msg[t, 1:2, :] = jnp.full((1, LANES), identity, jnp.float32)
 
@@ -107,7 +115,7 @@
             pooled = jnp.maximum(pooled, block[p * GROUP : (p + 1) * GROUP])
         label = jnp.zeros((GROUP, 1), jnp.int32)
         for t in range(GROUP):
-            label = jnp.where(sub == t, labels_ref[first + t], label)
+            label = jnp.where(sub == t, labels[first + t], label)
         correct = jnp.zeros((GROUP, 1), jnp.float32)
         rival = jnp.full((GROUP, 1), -1e30, jnp.float32)
         for k in range(classes):
@@ -170,25 +178,28 @@
     assert features.shape[0] == 1 and conv1_weight.shape[0] == 1 and n % GROUP == 0
     head = jnp.transpose(head_weight, (2, 0, 1))
     anywhere = pl.BlockSpec(memory_space=pl.ANY)
-    smem = pl.BlockSpec(memory_space=pltpu.SMEM)
+    hbm = pl.BlockSpec(memory_space=pltpu.HBM)
     vmem = pl.BlockSpec(memory_space=pltpu.VMEM)
     return pl.pallas_call(
         functools.partial(kernel, n),
         out_shape=(
-            jax.ShapeDtypeStruct((1, SUBSETS), jnp.float32),
-            jax.ShapeDtypeStruct((1,), jnp.float32),
-            jax.ShapeDtypeStruct((1,), jnp.float32),
+            pltpu.VMEM((1, SUBSETS), jnp.float32),
+            pltpu.VMEM((1,), jnp.float32),
+            pltpu.VMEM((1,), jnp.float32),
         ),
-        in_specs=[anywhere, smem, smem, anywhere, anywhere, anywhere],
+        in_specs=[anywhere, hbm, hbm, anywhere, anywhere, anywhere],
         out_specs=(vmem, vmem, vmem),
         scratch_shapes=[
             pltpu.VMEM((n, width, width, chans), features.dtype),
+            pltpu.SMEM(labels.shape, labels.dtype),
+            pltpu.SMEM(subset_ids.shape, subset_ids.dtype),
             pltpu.VMEM(conv1_weight.shape[1:], conv1_weight.dtype),
             pltpu.VMEM(conv2_weight.shape[1:], conv2_weight.dtype),
             pltpu.VMEM(head.shape, head.dtype),
             pltpu.VMEM((GROUP * width * width, offsets * chans), features.dtype),
             pltpu.VMEM((n, 2, LANES), jnp.float32),
             pltpu.VMEM((n, 2, LANES), jnp.float32),
+            pltpu.SemaphoreType.DMA((2,)),
             pltpu.SemaphoreType.DMA,
             pltpu.SemaphoreType.DMA((offsets,)),
             pltpu.SemaphoreType.DMA((offsets,)),

time: 24.9 us -> 21.7 us (0.87)
  between operations: 4.81 us -> 3.61 us
  Pallas kernels: 18.5 us -> 17.3 us
  local copies, waits for them, and re-layouts: 1.22 us -> 0.56 us
    pallas_call x1, Pallas kernels: 18.5 us -> 17.3 us  [shards(): pl.pallas_call(functools.partial(kernel, n), out_shape=(pltpu.VMEM((1, SU...]
    unnamed x1, local copies, waits for them, and re-layouts: 1.22 us -> 0.56 us
where the time goes in v2:
time: 21.7 us; the launch traced here: 21.5 us
  Pallas kernels  17.3 us (80%)
  between operations  3.61 us (17%)
  local copies, waits for them, and re-layouts  0.56 us (3%)
    pallas_call x1, Pallas kernels, shards(): pl.pallas_call(functools.partial(kernel, n), out_shape=(pltpu.VMEM((1, SU...  17.3 us
    unnamed x1, local copies, waits for them, and re-layouts  0.56 us

profile of v2, /device:TPU:0, one launch (start us, length us, event | category | flops | bytes accessed | tf_op | source)
XLA Modules:
  0.0 21.5 jit_solution(11131666663199839624)
XLA Ops:
  1.3 17.3 %shard_map.85 = (f32[1,256]{1,0:T(1,128)S(1)}, f32[1]{0:T(128)S(1)}, f32[1]{0:T(128)S(1)}) custom-call(bf16[1,4,4,512]{3,2,1,0:T(4,128)(2,1)} %feat_ref.1, s32[8]{0:T(128)} %labels_ref.1, s32[1]{0:T(128)S(6)} %copy.15.ids_ref, bf16[1,9,512,512]{3,2,1,0:T(8,128)(2,1)} %w1_ref.1, bf16[1,9,512,512]{3,2,1,0:T(8,128)(2,1)} %w2_ref.1, f32[10,1,512]{2,1,0:T(1,128)} %bitcast.1), custom_call_target="tpu_custom_call" | custom-call | tf_op jit(solution)/shard_map/pallas_call | solution.py:183
  18.7 0.6 %copy.12 = f32[1,256]{1,0:T(1,128)} copy(f32[1,256]{1,0:T(1,128)S(1)} %get-tuple-element.3) | data formatting | bytes 2048

commit v3 on v2

--- a/solution.py
+++ b/solution.py
@@ -15,8 +15,8 @@
 
 def kernel(
     n, feat_ref, labels_ref, ids_ref, w1_ref, w2_ref, head_ref,
-    data_ref, mean_ref, norm_ref,
-    gathered, labels, ids, w1, w2, head, lhs, msg, got,
+    got,
+    gathered, labels, ids, w1, w2, head, lhs, msg,
     small_sem, own_sem, w1_sem, w2_sem, head_sem, fsend, frecv, msend, mrecv,
 ):
     me = lax.axis_index("mp")
@@ -43,7 +43,8 @@
     ]
     head_copy = pltpu.make_async_copy(head_ref, head, head_sem)
 
-    peers = [lax.rem(me + j, n) for j in range(1, n)]
+    turn = 2 * lax.div(2 * me, n) - 1
+    peers = [lax.rem(me + turn * j + n, n) for j in range(1, n)]
     barrier = pltpu.get_barrier_semaphore()
     for peer in peers:
         pl.semaphore_signal(barrier, inc=1, device_id={"mp": peer}, device_id_type=MESH)
@@ -152,6 +153,9 @@
             device_id={"mp": peer}, device_id_type=MESH,
         ).wait_recv()
 
+
+def finish(got, data_ref, mean_ref, norm_ref):
+    n = got.shape[0]
     total = got[0, 0:1, :]
     for m in range(1, n):
         total = total + got[m, 0:1, :]
@@ -180,15 +184,11 @@
     anywhere = pl.BlockSpec(memory_space=pl.ANY)
     hbm = pl.BlockSpec(memory_space=pltpu.HBM)
     vmem = pl.BlockSpec(memory_space=pltpu.VMEM)
-    return pl.pallas_call(
+    got = pl.pallas_call(
         functools.partial(kernel, n),
-        out_shape=(
-            pltpu.VMEM((1, SUBSETS), jnp.float32),
-            pltpu.VMEM((1,), jnp.float32),
-            pltpu.VMEM((1,), jnp.float32),
-        ),
+        out_shape=pltpu.VMEM((n, 2, LANES), jnp.float32),
         in_specs=[anywhere, hbm, hbm, anywhere, anywhere, anywhere],
-        out_specs=(vmem, vmem, vmem),
+        out_specs=vmem,
         scratch_shapes=[
             pltpu.VMEM((n, width, width, chans), features.dtype),
             pltpu.SMEM(labels.shape, labels.dtype),
@@ -198,7 +198,6 @@
             pltpu.VMEM(head.shape, head.dtype),
             pltpu.VMEM((GROUP * width * width, offsets * chans), features.dtype),
             pltpu.VMEM((n, 2, LANES), jnp.float32),
-            pltpu.VMEM((n, 2, LANES), jnp.float32),
             pltpu.SemaphoreType.DMA((2,)),
             pltpu.SemaphoreType.DMA,
             pltpu.SemaphoreType.DMA((offsets,)),
@@ -213,6 +212,16 @@
             collective_id=0, has_side_effects=True, vmem_limit_bytes=60 * 1024 * 1024
         ),
     )(features, labels, subset_ids, conv1_weight, conv2_weight, head)
+    return pl.pallas_call(
+        finish,
+        out_shape=(
+            jax.ShapeDtypeStruct((1, SUBSETS), jnp.float32),
+            jax.ShapeDtypeStruct((1,), jnp.float32),
+            jax.ShapeDtypeStruct((1,), jnp.float32),
+        ),
+        in_specs=[vmem],
+        out_specs=(vmem, vmem, vmem),
+    )(pltpu.with_memory_space_constraint(got, pltpu.VMEM))
 
 
 def solution(mesh):

time: 21.7 us -> 18.3 us (0.84)
  between operations: 3.61 us -> 1.28 us
  local copies, waits for them, and re-layouts: 0.56 us -> 0 us
  Pallas kernels: 17.3 us -> 16.9 us
    unnamed x1 -> x0, local copies, waits for them, and re-layouts: 0.56 us -> none
    pallas_call x1 -> x2, Pallas kernels: 17.3 us -> 16.9 us  [the longest x1 16.2 us: shards(): pl.pallas_call(functools.partial(kernel, n), out_shape=pltpu.VMEM((n, 2,...]
where the time goes in v3:
time: 18.3 us; the launch traced here: 18.1 us
  Pallas kernels  16.9 us (92%)
  between operations  1.28 us (7%)
    pallas_call x1, Pallas kernels, shards(): pl.pallas_call(functools.partial(kernel, n), out_shape=pltpu.VMEM((n, 2,...  16.2 us
    pallas_call x1, Pallas kernels, shards(): pl.pallas_call(finish, out_shape=(jax.ShapeDtypeStruct((1, SUBSETS), jnp....  0.61 us

profile of v3, /device:TPU:0, one launch (start us, length us, event | category | flops | bytes accessed | tf_op | source)
XLA Modules:
  0.0 18.1 jit_solution(16020864761012277445)
XLA Ops:
  1.3 16.2 %shard_map.85.got = f32[8,2,128]{2,1,0:T(2,128)S(1)} custom-call(bf16[1,4,4,512]{3,2,1,0:T(4,128)(2,1)} %feat_ref.1, s32[8]{0:T(128)} %labels_ref.1, s32[1]{0:T(128)S(6)} %copy.9.ids_ref, bf16[1,9,512,512]{3,2,1,0:T(8,128)(2,1)} %w1_ref.1, bf16[1,9,512,512]{3,2,1,0:T(8,128)(2,1)} %w2_ref.1, f32[10,1,512]{2,1,0:T(1,128)} %bitcast.1), custom_call_target="tpu_custom_call" | custom-call | tf_op jit(solution)/shard_map/pallas_call | solution.py:187
  17.5 0.6 %shard_map.86 = (f32[1,256]{1,0:T(1,128)}, f32[1]{0:T(128)}, f32[1]{0:T(128)}) custom-call(f32[8,2,128]{2,1,0:T(2,128)S(1)} %shard_map.85.got), custom_call_target="tpu_custom_call" | custom-call | tf_op jit(solution)/shard_map/pallas_call | solution.py:215

commit v4 on v3

--- a/solution.py
+++ b/solution.py
@@ -16,10 +16,12 @@
 def kernel(
     n, feat_ref, labels_ref, ids_ref, w1_ref, w2_ref, head_ref,
     got,
-    gathered, labels, ids, w1, w2, head, lhs, msg,
-    small_sem, own_sem, w1_sem, w2_sem, head_sem, fsend, frecv, msend, mrecv,
+    mine, gathered, named, asked, labels, ids, w1, w2, head, lhs, msg,
+    small_sem, own_sem, name_sems, w1_sem, w2_sem, head_sem, fsend, frecv, msend, mrecv,
 ):
     me = lax.axis_index("mp")
+    dp = lax.axis_index("dp")
+    other = dp + 1 - 2 * lax.rem(dp, 2)
     width = feat_ref.shape[1]
     chans = feat_ref.shape[3]
     spots = width * width
@@ -27,10 +29,10 @@
     offsets = w1_ref.shape[1]
     classes = head_ref.shape[0]
 
-    own = pltpu.make_async_copy(feat_ref.at[0], gathered.at[me], own_sem)
+    own = pltpu.make_async_copy(feat_ref.at[0], mine, own_sem)
     own.start()
     small_copies = [
-        pltpu.make_async_copy(labels_ref, labels, small_sem.at[0]),
+        pltpu.make_async_copy(labels_ref, named, small_sem.at[0]),
         pltpu.make_async_copy(ids_ref, ids, small_sem.at[1]),
     ]
     for copy in small_copies:
@@ -44,10 +46,10 @@
     head_copy = pltpu.make_async_copy(head_ref, head, head_sem)
 
     turn = 2 * lax.div(2 * me, n) - 1
-    peers = [lax.rem(me + turn * j + n, n) for j in range(1, n)]
+    peers = [lax.rem(me + turn * j + n, n) for j in range(1, n)] + [me]
     barrier = pltpu.get_barrier_semaphore()
     for peer in peers:
-        pl.semaphore_signal(barrier, inc=1, device_id={"mp": peer}, device_id_type=MESH)
+        pl.semaphore_signal(barrier, inc=1, device_id={"mp": peer, "dp": other}, device_id_type=MESH)
     for copy in w1_copies:
         copy.start()
     for copy in w2_copies:
@@ -66,27 +68,37 @@
         msg[t, 1:2, :] = jnp.full((1, LANES), identity, jnp.float32)
 
     own.wait()
-    pl.semaphore_wait(barrier, n - 1)
+    pl.semaphore_wait(barrier, n)
     feature_sends = []
     for j, peer in enumerate(peers):
         copy = pltpu.make_async_remote_copy(
-            src_ref=gathered.at[me], dst_ref=gathered.at[me],
+            src_ref=mine, dst_ref=gathered.at[me],
             send_sem=fsend.at[j], recv_sem=frecv.at[me],
-            device_id={"mp": peer}, device_id_type=MESH,
+            device_id={"mp": peer, "dp": other}, device_id_type=MESH,
         )
         copy.start()
         feature_sends.append(copy)
+    name_send = pltpu.make_async_remote_copy(
+        src_ref=named, dst_ref=asked,
+        send_sem=name_sems.at[0], recv_sem=name_sems.at[1],
+        device_id={"mp": me, "dp": other}, device_id_type=MESH,
+    )
+    name_send.start()
 
     for copy in w1_copies:
         copy.wait()
     for copy in w2_copies:
         copy.wait()
     head_copy.wait()
+    name_send.wait()
+    asked_copy = pltpu.make_async_copy(asked, labels, small_sem.at[0])
+    asked_copy.start()
+    asked_copy.wait()
     for peer in peers:
         pltpu.make_async_remote_copy(
-            src_ref=gathered.at[peer], dst_ref=gathered.at[peer],
+            src_ref=mine, dst_ref=gathered.at[peer],
             send_sem=fsend.at[0], recv_sem=frecv.at[peer],
-            device_id={"mp": peer}, device_id_type=MESH,
+            device_id={"mp": peer, "dp": other}, device_id_type=MESH,
         ).wait_recv()
 
     def convolve(grid, kernel_ref):
@@ -137,11 +149,10 @@
         copy = pltpu.make_async_remote_copy(
             src_ref=msg.at[peer], dst_ref=got.at[me],
             send_sem=msend.at[j], recv_sem=mrecv.at[me],
-            device_id={"mp": peer}, device_id_type=MESH,
+            device_id={"mp": peer, "dp": other}, device_id_type=MESH,
         )
         copy.start()
         margin_sends.append(copy)
-    got[me] = msg[me]
     for copy in feature_sends:
         copy.wait_send()
     for copy in margin_sends:
@@ -150,7 +161,7 @@
         pltpu.make_async_remote_copy(
             src_ref=msg.at[peer], dst_ref=got.at[peer],
             send_sem=msend.at[0], recv_sem=mrecv.at[peer],
-            device_id={"mp": peer}, device_id_type=MESH,
+            device_id={"mp": peer, "dp": other}, device_id_type=MESH,
         ).wait_recv()
 
 
@@ -190,7 +201,10 @@
         in_specs=[anywhere, hbm, hbm, anywhere, anywhere, anywhere],
         out_specs=vmem,
         scratch_shapes=[
+            pltpu.VMEM((width, width, chans), features.dtype),
             pltpu.VMEM((n, width, width, chans), features.dtype),
+            pltpu.VMEM(labels.shape, labels.dtype),
+            pltpu.VMEM(labels.shape, labels.dtype),
             pltpu.SMEM(labels.shape, labels.dtype),
             pltpu.SMEM(subset_ids.shape, subset_ids.dtype),
             pltpu.VMEM(conv1_weight.shape[1:], conv1_weight.dtype),
@@ -200,6 +214,7 @@
             pltpu.VMEM((n, 2, LANES), jnp.float32),
             pltpu.SemaphoreType.DMA((2,)),
             pltpu.SemaphoreType.DMA,
+            pltpu.SemaphoreType.DMA((2,)),
             pltpu.SemaphoreType.DMA((offsets,)),
             pltpu.SemaphoreType.DMA((offsets,)),
             pltpu.SemaphoreType.DMA,
@@ -234,6 +249,7 @@
         P("mp", None, None),
     )
     out_specs = (P(("dp", "mp"), None), P(("dp", "mp")), P(("dp", "mp")))
+    assert mesh.shape["dp"] % 2 == 0
     return jax.shard_map(
         functools.partial(shards, mesh.shape["mp"]),
         mesh=mesh, in_specs=in_specs, out_specs=out_specs, check_vma=False,

time: 18.3 us -> 17.6 us (0.962)
  Pallas kernels: 16.9 us -> 16.2 us
    pallas_call x1, Pallas kernels: 16.2 us -> 15.6 us  [shards(): pl.pallas_call(functools.partial(kernel, n), out_shape=pltpu.VMEM((n, 2,...]
where the time goes in v4:
time: 17.6 us; the launch traced here: 17.5 us
  Pallas kernels  16.2 us (92%)
  between operations  1.28 us (7%)
    pallas_call x1, Pallas kernels, shards(): pl.pallas_call(functools.partial(kernel, n), out_shape=pltpu.VMEM((n, 2,...  15.6 us
    pallas_call x1, Pallas kernels, shards(): pl.pallas_call(finish, out_shape=(jax.ShapeDtypeStruct((1, SUBSETS), jnp....  0.61 us

profile of v4, /device:TPU:0, one launch (start us, length us, event | category | flops | bytes accessed | tf_op | source)
XLA Modules:
  0.0 17.5 jit_solution(11147113801178448654)
XLA Ops:
  1.3 15.6 %shard_map.85.got = f32[8,2,128]{2,1,0:T(2,128)S(1)} custom-call(bf16[1,4,4,512]{3,2,1,0:T(4,128)(2,1)} %feat_ref.1, s32[8]{0:T(128)} %labels_ref.1, s32[1]{0:T(128)S(6)} %copy.9.ids_ref, bf16[1,9,512,512]{3,2,1,0:T(8,128)(2,1)} %w1_ref.1, bf16[1,9,512,512]{3,2,1,0:T(8,128)(2,1)} %w2_ref.1, f32[10,1,512]{2,1,0:T(1,128)} %bitcast.1), custom_call_target="tpu_custom_call" | custom-call | tf_op jit(solution)/shard_map/pallas_call | solution.py:198
  16.9 0.6 %shard_map.86 = (f32[1,256]{1,0:T(1,128)}, f32[1]{0:T(128)}, f32[1]{0:T(128)}) custom-call(f32[8,2,128]{2,1,0:T(2,128)S(1)} %shard_map.85.got), custom_call_target="tpu_custom_call" | custom-call | tf_op jit(solution)/shard_map/pallas_call | solution.py:230

commit v5 on v4

--- a/solution.py
+++ b/solution.py
@@ -93,13 +93,14 @@
     name_send.wait()
     asked_copy = pltpu.make_async_copy(asked, labels, small_sem.at[0])
     asked_copy.start()
-    asked_copy.wait()
     for peer in peers:
         pltpu.make_async_remote_copy(
             src_ref=mine, dst_ref=gathered.at[peer],
             send_sem=fsend.at[0], recv_sem=frecv.at[peer],
             device_id={"mp": peer, "dp": other}, device_id_type=MESH,
         ).wait_recv()
+
+    asked_copy.wait()
 
     def convolve(grid, kernel_ref):
         blank = jnp.zeros((GROUP, chans), jnp.float32)
@@ -177,11 +178,11 @@
         spread = spread + centred * centred
     norm = jnp.sqrt(1.0 + spread / n)
     lane = lax.broadcasted_iota(jnp.int32, (1, LANES), 1).astype(jnp.float32)
+    scaled = [(got[m, 0:1, :] - mean) / norm for m in range(n)]
     for start in range(0, SUBSETS, LANES):
         acc = jnp.zeros((1, LANES), jnp.float32)
         for m in range(n):
-            scaled = (got[m, 0:1, :] - mean) / norm
-            acc = acc + jnp.where(got[m, 1:2, :] == lane + start, scaled, 0.0)
+            acc = acc + jnp.where(got[m, 1:2, :] == lane + start, scaled[m], 0.0)
         data_ref[:, start : start + LANES] = acc
     mean_ref[...] = mean[0, :1]
     norm_ref[...] = norm[0, :1]

time: 17.6 us -> 17.6 us (level)
  no operation moved by 1% of the time
where the time goes in v5:
time: 17.6 us; the launch traced here: 17.5 us
  Pallas kernels  16.2 us (92%)
  between operations  1.28 us (7%)
    pallas_call x1, Pallas kernels, shards(): pl.pallas_call(functools.partial(kernel, n), out_shape=pltpu.VMEM((n, 2,...  15.6 us
    pallas_call x1, Pallas kernels, shards(): pl.pallas_call(finish, out_shape=(jax.ShapeDtypeStruct((1, SUBSETS), jnp....  0.61 us

profile of v5, /device:TPU:0, one launch (start us, length us, event | category | flops | bytes accessed | tf_op | source)
XLA Modules:
  0.0 17.5 jit_solution(9643563743199003562)
XLA Ops:
  1.3 15.6 %shard_map.85.got = f32[8,2,128]{2,1,0:T(2,128)S(1)} custom-call(bf16[1,4,4,512]{3,2,1,0:T(4,128)(2,1)} %feat_ref.1, s32[8]{0:T(128)} %labels_ref.1, s32[1]{0:T(128)S(6)} %copy.9.ids_ref, bf16[1,9,512,512]{3,2,1,0:T(8,128)(2,1)} %w1_ref.1, bf16[1,9,512,512]{3,2,1,0:T(8,128)(2,1)} %w2_ref.1, f32[10,1,512]{2,1,0:T(1,128)} %bitcast.1), custom_call_target="tpu_custom_call" | custom-call | tf_op jit(solution)/shard_map/pallas_call | solution.py:199
  16.9 0.6 %shard_map.86 = (f32[1,256]{1,0:T(1,128)}, f32[1]{0:T(128)}, f32[1]{0:T(128)}) custom-call(f32[8,2,128]{2,1,0:T(2,128)S(1)} %shard_map.85.got), custom_call_target="tpu_custom_call" | custom-call | tf_op jit(solution)/shard_map/pallas_call | solution.py:231
